TPU v7x, 32 devices: a whole 2x2x4 slice. The times are simulated.
32 devices in a mesh: rep: 2 (over x), model: 4 (over z), vocab: 4 (over y, core).
Axes of the slice: x: 2, y: 2, z: 4, core: 2. Of those that a mesh axis runs over, the one named last changes fastest.
Arguments:
- hidden: bfloat16 [1024, 4096], P(('rep', 'model', 'vocab')), parts along dimension 0
- head_rows: bfloat16 [128256, 4096], P(('model', 'vocab'))
- allowed_ids: int32 [1024, 32], P(('rep', 'model', 'vocab')), parts along dimension 0
- valid_mask: int32 [1024, 32], P(('rep', 'model', 'vocab')), parts along dimension 0
- target_pos: int32 [1024], P(('rep', 'model', 'vocab')), parts along dimension 0
Outputs:
- output 1: float32 [1024, 32], P(('rep', 'model', 'vocab')), parts along dimension 0
- output 2: float32 [1024], P(('rep', 'model', 'vocab')), parts along dimension 0
There are 2 independent parts. A program takes and returns all parts, laid end to end along the dimension named above; an argument that names none is the same for every part.
All inputs are finite; a program needn't handle non-finite values.
Results may differ from a plain program's by a relative error of at most 0.001.
Values are sent between devices in bfloat16 or wider.
A program may use at most 1 GiB of HBM per device.

v0:
```python
import jax
import jax.numpy as jnp
from jax import lax
from jax.sharding import PartitionSpec as P

value_a11 = 0.5
OWNER_SHARE = 4


def masked_softmax(scores, is_valid, target_pos):
    scores = jnp.where(is_valid, scores, -jnp.inf)
    top_score = jnp.max(scores, axis=1, keepdims=True)
    log_norm = top_score[:, 0] + jnp.log(jnp.sum(jnp.exp(scores - top_score), axis=1))
    probs = jnp.where(is_valid, jnp.exp(scores - log_norm[:, None]), 0.0)
    picked_score = jnp.take_along_axis(scores, target_pos[:, None], axis=1)[:, 0]
    return probs, picked_score - log_norm


def solution(mesh):
    shard_axes = ('model', 'vocab')
    num_shards = mesh.shape['model'] * mesh.shape['vocab']
    row_spec = P(('rep', 'model', 'vocab'), None)
    vec_spec = P(('rep', 'model', 'vocab'))

    def local_step(hidden, head_rows, allowed_ids, valid_mask, target_pos):
        rows_loc, list_len = allowed_ids.shape
        shard_len = head_rows.shape[0]
        row_cap = list_len // OWNER_SHARE
        is_valid = valid_mask > 0
        shard_of = allowed_ids // shard_len
        offset = allowed_ids - shard_of * shard_len
        owner_shard = jnp.where(is_valid, shard_of, num_shards)
        own_hits = (owner_shard[:, :, None] == jnp.arange(num_shards, dtype=jnp.int32)).astype(jnp.int32)
        slot_rank = jnp.maximum(jnp.sum(jnp.cumsum(own_hits, axis=1) * own_hits, axis=2) - 1, 0)
        row_idx = jnp.arange(rows_loc, dtype=jnp.int32)[:, None]
        send_ids = jnp.zeros((num_shards, rows_loc, row_cap), jnp.int32)
        send_ids = send_ids.at[owner_shard, row_idx, slot_rank].set(offset, mode='drop')
        hidden_all = lax.all_gather(hidden, shard_axes)
        recv_ids = lax.all_to_all(send_ids, shard_axes, 0, 0)
        picked = head_rows[recv_ids]
        part_scores = jnp.einsum('sbcd,sbd->sbc', picked, hidden_all, preferred_element_type=jnp.float32)
        back_scores = lax.all_to_all(part_scores, shard_axes, 0, 0)
        safe_owner = jnp.minimum(owner_shard, num_shards - 1)
        scores = back_scores[safe_owner, row_idx, slot_rank] / value_a11
        return masked_softmax(scores, is_valid, target_pos)

    program = jax.shard_map(local_step, mesh=mesh, in_specs=(row_spec, P(shard_axes, None), row_spec, row_spec, vec_spec), out_specs=(row_spec, vec_spec), check_vma=False)
    return program
```

profile of v0, /device:TPU:0, one launch (start us, length us, event | category | flops | bytes accessed | tf_op | source)
XLA Modules:
  0.0 451.4 jit_solution(6056716633164663195)
XLA Ops:
  7.2 0.7 all-gather.3.cloned.1.call-update
  7.9 0.8 fusion.4
  8.7 0.1 reshape.79
  8.8 0.9 fusion.16
  9.8 0.7 multiply_reduce_fusion
  10.5 0.7 and_reduce_fusion
  11.4 4.3 scatter_custom_fusion
  15.7 0.1 reshape.53
  15.8 0.7 reshape.98
  16.5 7.4 %all-to-all-start = ((s32[16,1,256]{2,1,0:T(1,128)}), s32[16,1,256]{2,1,0:T(1,128)S(1)}, u32[]{:S(2)}, u32[]{:S(2)}) async-start(s32[16,1,256]{2,1,0:T(1,128)} %reshape.98), calls=%async_computation | async-start | bytes 32768 | tf_op jit(solution)/shard_map/all_to_all | solution.py:39
  23.9 0.7 fusion.14
  24.6 6.0 %all-to-all-done = s32[16,1,256]{2,1,0:T(1,128)S(1)} async-done(((s32[16,1,256]{2,1,0:T(1,128)}), s32[16,1,256]{2,1,0:T(1,128)S(1)}, u32[]{:S(2)}, u32[]{:S(2)}) %all-to-all-start) | async-done | bytes 16416 | tf_op jit(solution)/shard_map/all_to_all | solution.py:39
  30.6 0.5 broadcast.169
  31.1 0.7 reduce.4
  31.8 0.1 reshape.99
  31.9 0.1 copy.17
  32.0 0.2 reshape.57
  32.2 132.5 %gather_fusion = bf16[4096,4096]{1,0:T(8,128)(2,1)} fusion(bf16[8016,4096]{1,0:T(8,128)(2,1)} %param.6, s32[4096]{0:T(1024)S(1)} %broadcast_clamp_fusion), kind=kCustom, calls=%fused_computation | custom fusion | bytes 67125248 | tf_op jit(solution)/shard_map/gather | solution.py:40
  164.7 23.1 %fusion = f32[16,32,1,8]{3,2,1,0:T(1,128)S(1)} fusion(bf16[16,32,8,4096]{3,2,1,0:T(8,128)(2,1)} %bitcast.38, bf16[16,32,4096,1]{2,1,0,3:T(8,128)(2,1)} %bitcast.39), kind=kOutput, calls=%fused_computation.4 | convolution fusion | flops 33554432 | bytes 37765120 | tf_op jit(solution)/shard_map/sbcd,sbd->sbc/dot_general | solution.py:41
  187.8 0.1 copy.19
  187.9 0.7 reshape.100
  188.6 239.3 %all-to-all-start.1 = ((f32[16,1,256]{2,1,0:T(1,128)}), f32[16,1,256]{2,1,0:T(1,128)S(1)}, u32[]{:S(2)}, u32[]{:S(2)}) async-start(f32[16,1,256]{2,1,0:T(1,128)} %reshape.100), calls=%async_computation.1 | async-start | bytes 32768 | tf_op jit(solution)/shard_map/all_to_all | solution.py:42
  428.0 6.2 %all-to-all-done.1 = f32[16,1,256]{2,1,0:T(1,128)S(1)} async-done(((f32[16,1,256]{2,1,0:T(1,128)}), f32[16,1,256]{2,1,0:T(1,128)S(1)}, u32[]{:S(2)}, u32[]{:S(2)}) %all-to-all-start.1) | async-done | bytes 16416 | tf_op jit(solution)/shard_map/all_to_all | solution.py:42
  434.2 0.5 broadcast.170
  434.7 0.7 reduce.5
  435.4 0.1 reshape.101
  435.5 6.8 %gather_fusion.1 = f32[1024]{0:T(1024)S(1)} fusion(f32[16,32,8]{1,2,0:T(8,128)S(1)} %bitcast.37, s32[1024]{0:T(1024)S(1)} %reshape.63), kind=kCustom, calls=%fused_computation.1 | custom fusion | bytes 20480 | tf_op jit(solution)/shard_map/gather | solution.py:44
  442.4 0.1 fusion.15
  442.5 0.7 gather_fusion.2
  443.2 0.2 exponential_reduce_fusion
  443.4 0.5 fusion.13
  443.9 0.7 exponential_select_fusion
  (21 shorter events, 0.5 us)
Async XLA Ops:
  7.2 157.5 %all-gather.3.cloned.1.call-start = ((), (), s32[]{:S(2)}) async-start(), calls=%async_computation.2 | async-start | bytes 4456448 | tf_op jit(solution)/shard_map/all_gather | solution.py:38
  16.5 14.1 %all-to-all-start = ((s32[16,1,256]{2,1,0:T(1,128)}), s32[16,1,256]{2,1,0:T(1,128)S(1)}, u32[]{:S(2)}, u32[]{:S(2)}) async-start(s32[16,1,256]{2,1,0:T(1,128)} %reshape.98), calls=%async_computation | async-start | bytes 32768 | tf_op jit(solution)/shard_map/all_to_all | solution.py:39
  164.7 278.7 %copy-start = (s32[32]{0:T(128)S(1)}, s32[32]{0:T(128)}, u32[]{:S(2)}) copy-start(s32[32]{0:T(128)} %param.9) | copy-start | bytes 388
  188.6 245.6 %all-to-all-start.1 = ((f32[16,1,256]{2,1,0:T(1,128)}), f32[16,1,256]{2,1,0:T(1,128)S(1)}, u32[]{:S(2)}, u32[]{:S(2)}) async-start(f32[16,1,256]{2,1,0:T(1,128)} %reshape.100), calls=%async_computation.1 | async-start | bytes 32768 | tf_op jit(solution)/shard_map/all_to_all | solution.py:42
Sparse Core Ops, SparseCore 0:
  10.1 53.1 all-gather.2
where the time goes:
time: 457 us; the launch traced here: 451 us
  starting transfers between devices  247 us (54%)
  local copies, waits for them, and re-layouts  148 us (32%)
  matrix products  23.1 us (5%)
  between operations  14.2 us (3%)
  waiting for transfers between devices  12.9 us (3%)
  other arithmetic  6.74 us (1%)
    all_to_all x1, starting transfers between devices, local_step(): back_scores = lax.all_to_all(part_scores, shard_axes, 0, 0)  239 us
    gather x1, local copies, waits for them, and re-layouts, local_step(): picked = head_rows[recv_ids]  132 us
    dot_general x1, matrix products, local_step(): jnp.einsum('sbcd,sbd->sbc', picked, hidden_all, preferred_element_type=jn...  23.1 us
  transfers between devices with their start and end apart: 3, of which 2 were waited for; matrix products, arithmetic and copies ran while one was open for 32% of the time, Pallas kernels for 0%

commit v1 on v0

v1 whole, which is shorter than its diff:
```python
import functools

import jax
import jax.numpy as jnp
from jax import lax
from jax.experimental import pallas as pl
from jax.experimental.pallas import tpu as pltpu
from jax.sharding import PartitionSpec as P

TEMPERATURE = 0.5
MESH = pl.DeviceIdType.MESH
CONTRACT_LAST = (((1,), (1,)), ((), ()))
NUM_SHARDS = 16
NUM_PIECES = 8
NUM_SLOTS = 6
HEAD_BLOCK = 1008
SLOT_CAP = 8
LANES = 128
LEAD = 3


def kernel(shard_len, width, rows,
           tgt_ref, ids_ref, valid_ref, hidden_ref, head_ref,
           p_ref, lp_ref,
           head_buf, h_buf, square, turned, codes, offs_out, offs_in, acc, ret_in,
           head_sem, local_sem, recv_sem, own_sem, far_sem, relay_sem, hop_sem,
           offs_send, offs_recv, ret_send, ret_recv):
    depth = width // NUM_PIECES
    half = NUM_SHARDS // 2 * rows
    num_phases = 2 * NUM_PIECES
    z, v = lax.axis_index('model'), lax.axis_index('vocab')
    me = z * 4 + v
    z_near = z + 1 - 2 * lax.rem(z, 2)
    z_far = 2 * lax.rem(lax.div(z, 2) + 1, 2)
    v_other = lax.rem(v + 2, 4)
    v_sib = v + 1 - 2 * lax.rem(v, 2)
    v_sib_other = lax.rem(v_sib + 2, 4)

    def partner(step):
        return lax.rem(me + step, NUM_SHARDS)

    def device(shard):
        return {'model': lax.div(shard, 4), 'vocab': lax.rem(shard, 4)}

    barrier = pltpu.get_barrier_semaphore()
    for step in range(1, NUM_SHARDS):
        pl.semaphore_signal(barrier, inc=1, device_id=device(partner(step)), device_id_type=MESH)

    blocks = [(start, min(HEAD_BLOCK, shard_len - start)) for start in range(0, shard_len, HEAD_BLOCK)]

    def piece_of(phase):
        return lax.rem(phase + 2 * lax.div(phase, NUM_PIECES), NUM_PIECES)

    def head_copies(phase):
        cols = pl.ds(pl.multiple_of(piece_of(phase) * depth, depth), depth)
        slot = lax.rem(phase, NUM_SLOTS)
        return [pltpu.make_async_copy(head_ref.at[pl.ds(start, size), cols],
                                      head_buf.at[slot, pl.ds(start, size), :], head_sem.at[slot, i])
                for i, (start, size) in enumerate(blocks)]

    def block_of(shard, piece):
        return h_buf.at[piece, pl.ds(pl.multiple_of(shard * rows, rows), rows), :]

    local_copies = [pltpu.make_async_copy(hidden_ref.at[:, pl.ds(k * depth, depth)], block_of(me, k), local_sem.at[k])
                    for k in range(NUM_PIECES)]
    for copy in local_copies:
        copy.start()
    for phase in range(NUM_SLOTS):
        for copy in head_copies(phase):
            copy.start()

    square[...] = jnp.zeros_like(square)
    masked_ids = jnp.where(valid_ref[...] > 0, ids_ref[...], -1)
    for group in range(4):
        square[rows * group:rows * group + rows, 0:32] = masked_ids
    ids_t = jnp.transpose(square[...])[0:32, :]
    owner = jnp.zeros_like(ids_t)
    for s in range(1, NUM_SHARDS):
        owner = owner + jnp.where(ids_t >= s * shard_len, 1, 0)
    lane = lax.broadcasted_iota(jnp.int32, (32, LANES), 1)
    list_pos = lax.broadcasted_iota(jnp.int32, (32, LANES), 0)
    mine = (lane >= v * rows) & (lane < v * rows + rows) & (ids_t >= 0)
    owner = jnp.where(mine, owner, -1)
    offset1 = ids_t - owner * shard_len + 1
    rank = jnp.zeros_like(owner)
    for i in range(31):
        rank = rank + jnp.where((owner == owner[i:i + 1, :]) & (list_pos > i), 1, 0)
    code = jnp.where(mine, owner * SLOT_CAP + rank, -1)
    codes[0, :, :] = owner
    codes[1, :, :] = jnp.minimum(rank, SLOT_CAP - 1)
    slot_pos = lax.broadcasted_iota(jnp.int32, (SLOT_CAP, LANES), 0)
    tiles = [jnp.zeros((SLOT_CAP, LANES), jnp.int32) for _ in range(NUM_SHARDS)]
    for j in range(32):
        code_j, offset_j = code[j:j + 1, :], offset1[j:j + 1, :]
        for s in range(NUM_SHARDS):
            tiles[s] = jnp.where(code_j == slot_pos + s * SLOT_CAP, offset_j, tiles[s])
    for s in range(NUM_SHARDS):
        offs_out[s, :, :] = tiles[s]
    offs_in[me, :, :] = offs_out[me, :, :]
    acc[...] = jnp.zeros_like(acc)

    for copy in local_copies:
        copy.wait()
    pl.semaphore_wait(barrier, NUM_SHARDS - 1)

    def send_block(shard, piece, send_sem, to_z, to_v):
        return pltpu.make_async_remote_copy(
            src_ref=block_of(shard, piece), dst_ref=block_of(shard, piece), send_sem=send_sem,
            recv_sem=recv_sem.at[shard, piece], device_id={'model': to_z, 'vocab': to_v}, device_id_type=MESH)

    def arrived(shard, piece):
        send_block(shard, piece, recv_sem.at[shard, piece], z, v_sib).wait_recv()

    def own_sends(k):
        return [send_block(me, k, own_sem.at[0, k], z_near, v),
                send_block(me, k, own_sem.at[1, k], z, v_other),
                send_block(me, k, own_sem.at[2, k], z, v_sib)]

    def far_sends(k):
        return [send_block(me, k, far_sem.at[e, k], z_far + e, v) for e in range(2)]

    def send_offs(step):
        to = partner(step)
        return pltpu.make_async_remote_copy(
            src_ref=offs_out.at[to], dst_ref=offs_in.at[me], send_sem=offs_send.at[step], recv_sem=offs_recv.at[me],
            device_id=device(to), device_id_type=MESH)

    def pair_base(phase):
        return 2 * lax.rem(lax.div(z, 2) + lax.div(phase, NUM_PIECES), 2)

    def relay_sends(phase, e):
        shard, k = (pair_base(phase) + e) * 4 + v, piece_of(phase)
        return [send_block(shard, k, relay_sem.at[0, e, phase], z, v_other),
                send_block(shard, k, relay_sem.at[1, e, phase], z, v_sib)]

    def relay(phase):
        for e in range(2):
            @pl.when((phase < num_phases) & (pair_base(phase) + e != z))
            def _():
                arrived((pair_base(phase) + e) * 4 + v, piece_of(phase))
                for copy in relay_sends(phase, e):
                    copy.start()

    def hop_send(phase, e):
        return send_block((pair_base(phase) + e) * 4 + v_other, piece_of(phase), hop_sem.at[e, phase], z, v_sib)

    def hop(phase):
        @pl.when(phase < num_phases)
        def _():
            for e in range(2):
                arrived((pair_base(phase) + e) * 4 + v_other, piece_of(phase))
                hop_send(phase, e).start()

    def settle(phase):
        for e in range(2):
            arrived((pair_base(phase) + e) * 4 + v_sib, piece_of(phase))
            arrived((pair_base(phase) + e) * 4 + v_sib_other, piece_of(phase))

    def send_scores(step):
        to = partner(step)
        return pltpu.make_async_remote_copy(
            src_ref=acc.at[lax.div(to, 4)], dst_ref=ret_in.at[me], send_sem=ret_send.at[step], recv_sem=ret_recv.at[me],
            device_id=device(to), device_id_type=MESH)

    def near(step):
        return lax.div(partner(step), 8) == lax.div(me, 8)

    for copy in own_sends(0):
        copy.start()
    for step in range(1, NUM_SHARDS):
        send_offs(step).start()
    for k in range(1, NUM_PIECES):
        for copy in own_sends(k):
            copy.start()
    for phase in range(LEAD):
        relay(phase)
    hop(0)

    def wait_offs(step):
        src = partner(step)
        pltpu.make_async_remote_copy(
            src_ref=offs_out.at[src], dst_ref=offs_in.at[src], send_sem=offs_send.at[step], recv_sem=offs_recv.at[src],
            device_id=device(src), device_id_type=MESH).wait_recv()

    for step in range(1, NUM_SHARDS):
        wait_offs(step)

    def run_phase(phase, carry):
        @pl.when(phase < NUM_PIECES)
        def _():
            for copy in far_sends(piece_of(phase + NUM_PIECES)):
                copy.start()

        relay(phase + LEAD)
        hop(phase + 1)
        settle(phase)

        @pl.when((phase < NUM_PIECES) | (phase >= NUM_PIECES + NUM_SLOTS))
        def _():
            for copy in head_copies(phase):
                copy.wait()

        slot = lax.rem(phase, NUM_SLOTS)
        base = pair_base(phase)
        hidden = h_buf[piece_of(phase), pl.ds(pl.multiple_of(base * 4 * rows, half), half), :]
        offsets = []
        for l in range(2):
            total = offs_in[(base + l) * 4, :, :]
            for u in range(1, 4):
                total = total + offs_in[(base + l) * 4 + u, :, :]
            offsets.append(total - 1)
        sums = [acc[base + l, :, :] for l in range(2)]
        for start, size in blocks:
            scores = lax.dot_general(head_buf[slot, start:start + size, :], hidden, CONTRACT_LAST,
                                     preferred_element_type=jnp.float32)
            for l in range(2):
                low = offsets[l] & 7
                high = (offsets[l] >> 3) - start // 8
                found = jnp.zeros((SLOT_CAP, LANES), jnp.float32)
                for g in range(size // 8):
                    tile = scores[8 * g:8 * g + 8, LANES * l:LANES * l + LANES]
                    found = jnp.where(high == g, jnp.take_along_axis(tile, low, axis=0), found)
                sums[l] = sums[l] + found
        for l in range(2):
            acc[base + l, :, :] = sums[l]

        @pl.when((phase < NUM_PIECES - NUM_SLOTS) | ((phase >= NUM_PIECES) & (phase < 2 * NUM_PIECES - NUM_SLOTS)))
        def _():
            for copy in head_copies(phase + NUM_SLOTS):
                copy.start()

        @pl.when(phase == NUM_PIECES)
        def _():
            for step in range(1, NUM_SHARDS):
                @pl.when(near(step))
                def _():
                    send_scores(step).start()

        return carry

    lax.fori_loop(0, num_phases, run_phase, 0)

    for step in range(1, NUM_SHARDS):
        @pl.when(jnp.logical_not(near(step)))
        def _():
            send_scores(step).start()
    ret_in[me, :, :] = acc[z, :, :]

    row_pos = lax.broadcasted_iota(jnp.int32, (rows, 32), 0)
    target = jnp.zeros((rows, 32), jnp.int32)
    for b in range(rows):
        target = jnp.where(row_pos == b, tgt_ref[b], target)

    def end_piece(k, carry):
        for copy in own_sends(k) + far_sends(k):
            copy.wait_send()
        return carry

    lax.fori_loop(0, NUM_PIECES, end_piece, 0)

    def end_phase(phase, carry):
        for e in range(2):
            @pl.when(pair_base(phase) + e != z)
            def _():
                for copy in relay_sends(phase, e):
                    copy.wait_send()
            hop_send(phase, e).wait_send()
        return carry

    lax.fori_loop(0, num_phases, end_phase, 0)
    for step in range(1, NUM_SHARDS):
        send_offs(step).wait_send()
        send_scores(step).wait_send()
    for step in range(1, NUM_SHARDS):
        src = partner(step)
        pltpu.make_async_remote_copy(
            src_ref=acc.at[0], dst_ref=ret_in.at[src], send_sem=ret_send.at[step], recv_sem=ret_recv.at[src],
            device_id=device(src), device_id_type=MESH).wait_recv()

    turned[...] = jnp.zeros_like(turned)
    for q in range(4):
        owner_q, rank_q = codes[0, 8 * q:8 * q + 8, :], codes[1, 8 * q:8 * q + 8, :]
        picked = jnp.zeros((8, LANES), jnp.float32)
        for s in range(NUM_SHARDS):
            picked = jnp.where(owner_q == s, jnp.take_along_axis(ret_in[s, :, :], rank_q, axis=0), picked)
        turned[8 * q:8 * q + 8, :] = picked
    turned[...] = jnp.transpose(turned[...])
    raw = turned[pl.ds(pl.multiple_of(v * rows, rows), rows), :][:, 0:32]
    is_valid = valid_ref[...] > 0
    logits = jnp.where(is_valid, raw / TEMPERATURE, -jnp.inf)
    top = jnp.max(logits, axis=1, keepdims=True)
    log_norm = top + jnp.log(jnp.sum(jnp.exp(logits - top), axis=1, keepdims=True))
    p_ref[...] = jnp.where(is_valid, jnp.exp(logits - log_norm), 0.0)
    col_pos = lax.broadcasted_iota(jnp.int32, (rows, 32), 1)
    chosen = jnp.sum(jnp.where(col_pos == target, logits, 0.0), axis=1, keepdims=True)
    turned[0:rows, :] = jnp.broadcast_to(chosen - log_norm, (rows, LANES))
    lp_ref[...] = jnp.transpose(turned[...])[0:1, 0:rows]


def solution(mesh):
    shard_axes = ('model', 'vocab')
    row_spec = P(('rep', 'model', 'vocab'), None)
    vec_spec = P(('rep', 'model', 'vocab'))

    def local_step(hidden, head_rows, allowed_ids, valid_mask, target_pos):
        rows, width = hidden.shape
        shard_len = head_rows.shape[0]
        depth = width // NUM_PIECES
        num_blocks = -(-shard_len // HEAD_BLOCK)
        dma = pltpu.SemaphoreType.DMA
        tile = (SLOT_CAP, LANES)
        p, lp = pl.pallas_call(
            functools.partial(kernel, shard_len, width, rows),
            out_shape=(jax.ShapeDtypeStruct((rows, 32), jnp.float32), jax.ShapeDtypeStruct((1, rows), jnp.float32)),
            in_specs=[pl.BlockSpec(memory_space=pltpu.SMEM), pl.BlockSpec(memory_space=pltpu.VMEM),
                      pl.BlockSpec(memory_space=pltpu.VMEM), pl.BlockSpec(memory_space=pl.ANY),
                      pl.BlockSpec(memory_space=pl.ANY)],
            out_specs=(pl.BlockSpec(memory_space=pltpu.VMEM), pl.BlockSpec(memory_space=pltpu.VMEM)),
            scratch_shapes=[
                pltpu.VMEM((NUM_SLOTS, shard_len, depth), jnp.bfloat16),
                pltpu.VMEM((NUM_PIECES, NUM_SHARDS * rows, depth), jnp.bfloat16),
                pltpu.VMEM((LANES, LANES), jnp.int32),
                pltpu.VMEM((LANES, LANES), jnp.float32),
                pltpu.VMEM((2, 32, LANES), jnp.int32),
                pltpu.VMEM((NUM_SHARDS,) + tile, jnp.int32),
                pltpu.VMEM((NUM_SHARDS,) + tile, jnp.int32),
                pltpu.VMEM((4,) + tile, jnp.float32),
                pltpu.VMEM((NUM_SHARDS,) + tile, jnp.float32),
                dma((NUM_SLOTS, num_blocks)), dma((NUM_PIECES,)), dma((NUM_SHARDS, NUM_PIECES)),
                dma((3, NUM_PIECES)), dma((2, NUM_PIECES)), dma((2, 2, 2 * NUM_PIECES)), dma((2, 2 * NUM_PIECES)),
                dma((NUM_SHARDS,)), dma((NUM_SHARDS,)), dma((NUM_SHARDS,)), dma((NUM_SHARDS,)),
            ],
            compiler_params=pltpu.CompilerParams(collective_id=0, has_side_effects=True, vmem_limit_bytes=67043328),
        )(target_pos, allowed_ids, valid_mask, hidden, head_rows)
        return p, lp.reshape(rows)

    return jax.shard_map(local_step, mesh=mesh, in_specs=(row_spec, P(shard_axes, None), row_spec, row_spec, vec_spec),
                         out_specs=(row_spec, vec_spec), check_vma=False)
```

time: 457 us -> 80.4 us (0.18); the launches traced: 451 us -> 80 us
  starting transfers between devices: 247 us -> 0 us
  local copies, waits for them, and re-layouts: 148 us -> 2.46 us
  Pallas kernels: 0 us -> 76.9 us
  matrix products: 23.1 us -> 0 us
  between operations: 14.2 us -> 0.64 us
  waiting for transfers between devices: 12.9 us -> 0 us
  other arithmetic: 6.74 us -> 0 us
    all_to_all x2 -> x0, starting transfers between devices: 247 us -> none  [the longest x1 239 us: local_step(): back_scores = lax.all_to_all(part_scores, shard_axes, 0, 0)]
    gather x3 -> x0, local copies, waits for them, and re-layouts: 140 us -> none  [the longest x1 132 us: local_step(): picked = head_rows[recv_ids]]
    pallas_call x0 -> x1, Pallas kernels: none -> 76.9 us  [local_step(): pl.pallas_call(functools.partial(kernel, shard_len, width, rows), out_sha...]
    dot_general x1 -> x0, matrix products: 23.1 us -> none  [local_step(): jnp.einsum('sbcd,sbd->sbc', picked, hidden_all, preferred_element_type=jn...]
    all_to_all x2 -> x0, waiting for transfers between devices: 12.2 us -> none  [the longest x1 6.24 us: local_step(): back_scores = lax.all_to_all(part_scores, shard_axes, 0, 0)]
  transfers between devices with their start and end apart: 3 -> 0, of which waited for: 2 -> 0; matrix products, arithmetic and copies ran while one was open for 32% -> 0% of each run, Pallas kernels for 0% -> 0%
where the time goes in v1:
time: 80.4 us; the launch traced here: 80 us
  Pallas kernels  76.9 us (96%)
  local copies, waits for them, and re-layouts  2.46 us (3%)
    pallas_call x1, Pallas kernels, local_step(): pl.pallas_call(functools.partial(kernel, shard_len, width, rows), out_sha...  76.9 us
    unnamed x2, local copies, waits for them, and re-layouts  2.46 us

profile of v1, /device:TPU:0, one launch (start us, length us, event | category | flops | bytes accessed | tf_op | source)
XLA Modules:
  0.0 80.0 jit_solution(7313045375431723075)
XLA Ops:
  0.6 76.9 %shard_map.68 = (f32[32,32]{1,0:T(8,128)}, f32[1,32]{1,0:T(1,128)}) custom-call(s32[32]{0:T(128)} %tgt_ref.1, s32[32,32]{1,0:T(8,128)} %ids_ref.1, s32[32,32]{1,0:T(8,128)} %valid_ref.1, bf16[32,4096]{1,0:T(8,128)(2,1)} %hidden_ref.1, bf16[8016,4096]{1,0:T(8,128)(2,1)} %head_ref.1), custom_call_target="tpu_custom_call" | custom-call | tf_op jit(solution)/shard_map/pallas_call | solution.py:312
  77.6 1.3 %copy.9 = f32[32,32]{1,0:T(8,128)} copy(f32[32,32]{1,0:T(8,128)} %get-tuple-element.8) | data formatting | bytes 8192
  78.9 1.1 %copy.10 = f32[32]{0:T(128)} copy(f32[32]{0:T(128)} %bitcast.1) | data formatting | bytes 256

commit v2 on v1

--- a/solution.py
+++ b/solution.py
@@ -20,8 +20,9 @@
 
 
 def kernel(shard_len, width, rows,
-           tgt_ref, ids_ref, valid_ref, hidden_ref, head_ref,
-           p_ref, lp_ref,
+           tgt_hbm, ids_hbm, valid_hbm, hidden_ref, head_ref,
+           p_hbm, lp_hbm,
+           tgt_ref, ids_ref, valid_ref, p_ref, lp_ref, small_sem,
            head_buf, h_buf, square, turned, codes, offs_out, offs_in, acc, ret_in,
            head_sem, local_sem, recv_sem, own_sem, far_sem, relay_sem, hop_sem,
            offs_send, offs_recv, ret_send, ret_recv):
@@ -63,11 +64,88 @@
 
     local_copies = [pltpu.make_async_copy(hidden_ref.at[:, pl.ds(k * depth, depth)], block_of(me, k), local_sem.at[k])
                     for k in range(NUM_PIECES)]
-    for copy in local_copies:
+    small_copies = [pltpu.make_async_copy(src, dst, small_sem.at[i]) for i, (src, dst) in enumerate(
+        ((ids_hbm, ids_ref), (valid_hbm, valid_ref), (tgt_hbm, tgt_ref)))]
+    out_copies = [pltpu.make_async_copy(src, dst, small_sem.at[3 + i]) for i, (src, dst) in enumerate(
+        ((p_ref, p_hbm), (lp_ref, lp_hbm)))]
+    for copy in local_copies[:LEAD] + small_copies + local_copies[LEAD:]:
         copy.start()
     for phase in range(NUM_SLOTS):
         for copy in head_copies(phase):
+            copy.start(priority=1)
+
+    pl.semaphore_wait(barrier, NUM_SHARDS - 1)
+
+    def send_block(shard, piece, send_sem, to_z, to_v):
+        return pltpu.make_async_remote_copy(
+            src_ref=block_of(shard, piece), dst_ref=block_of(shard, piece), send_sem=send_sem,
+            recv_sem=recv_sem.at[shard, piece], device_id={'model': to_z, 'vocab': to_v}, device_id_type=MESH)
+
+    def arrived(shard, piece):
+        send_block(shard, piece, recv_sem.at[shard, piece], z, v_sib).wait_recv()
+
+    def line_send(k):
+        return send_block(me, k, own_sem.at[0, k], z_near, v)
+
+    def side_sends(k):
+        return [send_block(me, k, own_sem.at[1, k], z, v_other), send_block(me, k, own_sem.at[2, k], z, v_sib)]
+
+    def far_sends(k):
+        return [send_block(me, k, far_sem.at[e, k], z_far + e, v) for e in range(2)]
+
+    def send_offs(step):
+        to = partner(step)
+        return pltpu.make_async_remote_copy(
+            src_ref=offs_out.at[to], dst_ref=offs_in.at[me], send_sem=offs_send.at[step], recv_sem=offs_recv.at[me],
+            device_id=device(to), device_id_type=MESH)
+
+    def pair_base(phase):
+        return 2 * lax.rem(lax.div(z, 2) + lax.div(phase, NUM_PIECES), 2)
+
+    def relay_sends(phase, e):
+        shard, k = (pair_base(phase) + e) * 4 + v, piece_of(phase)
+        return [send_block(shard, k, relay_sem.at[0, e, phase], z, v_other),
+                send_block(shard, k, relay_sem.at[1, e, phase], z, v_sib)]
+
+    def relay(phase):
+        for e in range(2):
+            @pl.when((phase < num_phases) & (pair_base(phase) + e != z))
+            def _():
+                arrived((pair_base(phase) + e) * 4 + v, piece_of(phase))
+                for copy in relay_sends(phase, e):
+                    copy.start()
+
+    def hop_send(phase, e):
+        return send_block((pair_base(phase) + e) * 4 + v_other, piece_of(phase), hop_sem.at[e, phase], z, v_sib)
+
+    def hop(phase):
+        @pl.when(phase < num_phases)
+        def _():
+            for e in range(2):
+                arrived((pair_base(phase) + e) * 4 + v_other, piece_of(phase))
+                hop_send(phase, e).start()
+
+    def settle(phase):
+        for e in range(2):
+            arrived((pair_base(phase) + e) * 4 + v_sib, piece_of(phase))
+            arrived((pair_base(phase) + e) * 4 + v_sib_other, piece_of(phase))
+
+    def send_scores(step):
+        to = partner(step)
+        return pltpu.make_async_remote_copy(
+            src_ref=acc.at[lax.div(to, 4)], dst_ref=ret_in.at[me], send_sem=ret_send.at[step], recv_sem=ret_recv.at[me],
+            device_id=device(to), device_id_type=MESH)
+
+    def near(step):
+        return lax.div(partner(step), 8) == lax.div(me, 8)
+
+    for k in range(LEAD):
+        local_copies[k].wait()
+        line_send(k).start()
+        for copy in side_sends(k):
             copy.start()
+    for copy in small_copies:
+        copy.wait()
 
     square[...] = jnp.zeros_like(square)
     masked_ids = jnp.where(valid_ref[...] > 0, ids_ref[...], -1)
@@ -99,81 +177,15 @@
     offs_in[me, :, :] = offs_out[me, :, :]
     acc[...] = jnp.zeros_like(acc)
 
-    for copy in local_copies:
-        copy.wait()
-    pl.semaphore_wait(barrier, NUM_SHARDS - 1)
-
-    def send_block(shard, piece, send_sem, to_z, to_v):
-        return pltpu.make_async_remote_copy(
-            src_ref=block_of(shard, piece), dst_ref=block_of(shard, piece), send_sem=send_sem,
-            recv_sem=recv_sem.at[shard, piece], device_id={'model': to_z, 'vocab': to_v}, device_id_type=MESH)
-
-    def arrived(shard, piece):
-        send_block(shard, piece, recv_sem.at[shard, piece], z, v_sib).wait_recv()
-
-    def own_sends(k):
-        return [send_block(me, k, own_sem.at[0, k], z_near, v),
-                send_block(me, k, own_sem.at[1, k], z, v_other),
-                send_block(me, k, own_sem.at[2, k], z, v_sib)]
-
-    def far_sends(k):
-        return [send_block(me, k, far_sem.at[e, k], z_far + e, v) for e in range(2)]
-
-    def send_offs(step):
-        to = partner(step)
-        return pltpu.make_async_remote_copy(
-            src_ref=offs_out.at[to], dst_ref=offs_in.at[me], send_sem=offs_send.at[step], recv_sem=offs_recv.at[me],
-            device_id=device(to), device_id_type=MESH)
-
-    def pair_base(phase):
-        return 2 * lax.rem(lax.div(z, 2) + lax.div(phase, NUM_PIECES), 2)
-
-    def relay_sends(phase, e):
-        shard, k = (pair_base(phase) + e) * 4 + v, piece_of(phase)
-        return [send_block(shard, k, relay_sem.at[0, e, phase], z, v_other),
-                send_block(shard, k, relay_sem.at[1, e, phase], z, v_sib)]
-
-    def relay(phase):
-        for e in range(2):
-            @pl.when((phase < num_phases) & (pair_base(phase) + e != z))
-            def _():
-                arrived((pair_base(phase) + e) * 4 + v, piece_of(phase))
-                for copy in relay_sends(phase, e):
-                    copy.start()
-
-    def hop_send(phase, e):
-        return send_block((pair_base(phase) + e) * 4 + v_other, piece_of(phase), hop_sem.at[e, phase], z, v_sib)
-
-    def hop(phase):
-        @pl.when(phase < num_phases)
-        def _():
-            for e in range(2):
-                arrived((pair_base(phase) + e) * 4 + v_other, piece_of(phase))
-                hop_send(phase, e).start()
-
-    def settle(phase):
-        for e in range(2):
-            arrived((pair_base(phase) + e) * 4 + v_sib, piece_of(phase))
-            arrived((pair_base(phase) + e) * 4 + v_sib_other, piece_of(phase))
-
-    def send_scores(step):
-        to = partner(step)
-        return pltpu.make_async_remote_copy(
-            src_ref=acc.at[lax.div(to, 4)], dst_ref=ret_in.at[me], send_sem=ret_send.at[step], recv_sem=ret_recv.at[me],
-            device_id=device(to), device_id_type=MESH)
-
-    def near(step):
-        return lax.div(partner(step), 8) == lax.div(me, 8)
-
-    for copy in own_sends(0):
-        copy.start()
     for step in range(1, NUM_SHARDS):
         send_offs(step).start()
-    for k in range(1, NUM_PIECES):
-        for copy in own_sends(k):
-            copy.start()
+    for k in range(LEAD, NUM_PIECES):
+        local_copies[k].wait()
+        line_send(k).start()
     for phase in range(LEAD):
         relay(phase)
+        for copy in side_sends(LEAD + phase):
+            copy.start()
     hop(0)
 
     def wait_offs(step):
@@ -192,6 +204,12 @@
                 copy.start()
 
         relay(phase + LEAD)
+
+        @pl.when(phase < NUM_PIECES - 2 * LEAD)
+        def _():
+            for copy in side_sends(phase + 2 * LEAD):
+                copy.start()
+
         hop(phase + 1)
         settle(phase)
 
@@ -227,7 +245,7 @@
         @pl.when((phase < NUM_PIECES - NUM_SLOTS) | ((phase >= NUM_PIECES) & (phase < 2 * NUM_PIECES - NUM_SLOTS)))
         def _():
             for copy in head_copies(phase + NUM_SLOTS):
-                copy.start()
+                copy.start(priority=1)
 
         @pl.when(phase == NUM_PIECES)
         def _():
@@ -252,7 +270,7 @@
         target = jnp.where(row_pos == b, tgt_ref[b], target)
 
     def end_piece(k, carry):
-        for copy in own_sends(k) + far_sends(k):
+        for copy in [line_send(k)] + side_sends(k) + far_sends(k):
             copy.wait_send()
         return carry
 
@@ -291,10 +309,14 @@
     top = jnp.max(logits, axis=1, keepdims=True)
     log_norm = top + jnp.log(jnp.sum(jnp.exp(logits - top), axis=1, keepdims=True))
     p_ref[...] = jnp.where(is_valid, jnp.exp(logits - log_norm), 0.0)
+    out_copies[0].start()
     col_pos = lax.broadcasted_iota(jnp.int32, (rows, 32), 1)
     chosen = jnp.sum(jnp.where(col_pos == target, logits, 0.0), axis=1, keepdims=True)
     turned[0:rows, :] = jnp.broadcast_to(chosen - log_norm, (rows, LANES))
     lp_ref[...] = jnp.transpose(turned[...])[0:1, 0:rows]
+    out_copies[1].start()
+    for copy in out_copies:
+        copy.wait()
 
 
 def solution(mesh):
@@ -312,11 +334,15 @@
         p, lp = pl.pallas_call(
             functools.partial(kernel, shard_len, width, rows),
             out_shape=(jax.ShapeDtypeStruct((rows, 32), jnp.float32), jax.ShapeDtypeStruct((1, rows), jnp.float32)),
-            in_specs=[pl.BlockSpec(memory_space=pltpu.SMEM), pl.BlockSpec(memory_space=pltpu.VMEM),
-                      pl.BlockSpec(memory_space=pltpu.VMEM), pl.BlockSpec(memory_space=pl.ANY),
-                      pl.BlockSpec(memory_space=pl.ANY)],
-            out_specs=(pl.BlockSpec(memory_space=pltpu.VMEM), pl.BlockSpec(memory_space=pltpu.VMEM)),
+            in_specs=[pl.BlockSpec(memory_space=pl.ANY)] * 5,
+            out_specs=(pl.BlockSpec(memory_space=pl.ANY),) * 2,
             scratch_shapes=[
+                pltpu.SMEM((rows,), jnp.int32),
+                pltpu.VMEM((rows, 32), jnp.int32),
+                pltpu.VMEM((rows, 32), jnp.int32),
+                pltpu.VMEM((rows, 32), jnp.float32),
+                pltpu.VMEM((1, rows), jnp.float32),
+                dma((5,)),
                 pltpu.VMEM((NUM_SLOTS, shard_len, depth), jnp.bfloat16),
                 pltpu.VMEM((NUM_PIECES, NUM_SHARDS * rows, depth), jnp.bfloat16),
                 pltpu.VMEM((LANES, LANES), jnp.int32),

time: 80.4 us -> 64.6 us (0.80)
  Pallas kernels: 76.9 us -> 61.3 us
    pallas_call x1, Pallas kernels: 76.9 us -> 61.3 us  [local_step(): pl.pallas_call(functools.partial(kernel, shard_len, width, rows), out_sha...]
where the time goes in v2:
time: 64.6 us; the launch traced here: 64.4 us
  Pallas kernels  61.3 us (95%)
  local copies, waits for them, and re-layouts  2.46 us (4%)
    pallas_call x1, Pallas kernels, local_step(): pl.pallas_call(functools.partial(kernel, shard_len, width, rows), out_sha...  61.3 us
    unnamed x2, local copies, waits for them, and re-layouts  2.46 us

profile of v2, /device:TPU:0, one launch (start us, length us, event | category | flops | bytes accessed | tf_op | source)
XLA Modules:
  0.0 64.4 jit_solution(18188240329583858909)
XLA Ops:
  0.6 61.3 %shard_map.68 = (f32[32,32]{1,0:T(8,128)}, f32[1,32]{1,0:T(1,128)}) custom-call(s32[32]{0:T(128)} %tgt_hbm.1, s32[32,32]{1,0:T(8,128)} %ids_hbm.1, s32[32,32]{1,0:T(8,128)} %valid_hbm.1, bf16[32,4096]{1,0:T(8,128)(2,1)} %hidden_ref.1, bf16[8016,4096]{1,0:T(8,128)(2,1)} %head_ref.1), custom_call_target="tpu_custom_call" | custom-call | tf_op jit(solution)/shard_map/pallas_call | solution.py:334
  61.9 1.3 %copy.9 = f32[32,32]{1,0:T(8,128)} copy(f32[32,32]{1,0:T(8,128)} %get-tuple-element.8) | data formatting | bytes 8192
  63.2 1.1 %copy.10 = f32[32]{0:T(128)} copy(f32[32]{0:T(128)} %bitcast.1) | data formatting | bytes 256

commit v3 on v2

--- a/solution.py
+++ b/solution.py
@@ -50,11 +50,14 @@
     blocks = [(start, min(HEAD_BLOCK, shard_len - start)) for start in range(0, shard_len, HEAD_BLOCK)]
 
     def piece_of(phase):
-        return lax.rem(phase + 2 * lax.div(phase, NUM_PIECES), NUM_PIECES)
+        return lax.rem(phase + lax.div(phase, 7), 7) * (1 - lax.div(phase, 14)) + 7 * lax.div(phase, 14)
+
+    def slot_of(phase):
+        return lax.rem(phase - lax.div(phase, 15), NUM_SLOTS)
 
     def head_copies(phase):
         cols = pl.ds(pl.multiple_of(piece_of(phase) * depth, depth), depth)
-        slot = lax.rem(phase, NUM_SLOTS)
+        slot = slot_of(phase)
         return [pltpu.make_async_copy(head_ref.at[pl.ds(start, size), cols],
                                       head_buf.at[slot, pl.ds(start, size), :], head_sem.at[slot, i])
                 for i, (start, size) in enumerate(blocks)]
@@ -100,7 +103,8 @@
             device_id=device(to), device_id_type=MESH)
 
     def pair_base(phase):
-        return 2 * lax.rem(lax.div(z, 2) + lax.div(phase, NUM_PIECES), 2)
+        far = lax.div(phase, 7) - lax.div(phase, 14) - lax.div(phase, 15)
+        return 2 * lax.rem(lax.div(z, 2) + far, 2)
 
     def relay_sends(phase, e):
         shard, k = (pair_base(phase) + e) * 4 + v, piece_of(phase)
@@ -178,10 +182,23 @@
     acc[...] = jnp.zeros_like(acc)
 
     for step in range(1, NUM_SHARDS):
-        send_offs(step).start()
+        @pl.when(near(step))
+        def _():
+            send_offs(step).start()
+
     for k in range(LEAD, NUM_PIECES):
         local_copies[k].wait()
-        line_send(k).start()
+    for i in range(NUM_PIECES):
+        if LEAD + i < NUM_PIECES - 1:
+            line_send(LEAD + i).start()
+        for copy in far_sends(piece_of(7 + i)):
+            copy.start()
+    line_send(NUM_PIECES - 1).start()
+    for step in range(1, NUM_SHARDS):
+        @pl.when(jnp.logical_not(near(step)))
+        def _():
+            send_offs(step).start()
+
     for phase in range(LEAD):
         relay(phase)
         for copy in side_sends(LEAD + phase):
@@ -195,30 +212,12 @@
             device_id=device(src), device_id_type=MESH).wait_recv()
 
     for step in range(1, NUM_SHARDS):
-        wait_offs(step)
-
-    def run_phase(phase, carry):
-        @pl.when(phase < NUM_PIECES)
-        def _():
-            for copy in far_sends(piece_of(phase + NUM_PIECES)):
-                copy.start()
-
-        relay(phase + LEAD)
-
-        @pl.when(phase < NUM_PIECES - 2 * LEAD)
-        def _():
-            for copy in side_sends(phase + 2 * LEAD):
-                copy.start()
-
-        hop(phase + 1)
-        settle(phase)
-
-        @pl.when((phase < NUM_PIECES) | (phase >= NUM_PIECES + NUM_SLOTS))
-        def _():
-            for copy in head_copies(phase):
-                copy.wait()
-
-        slot = lax.rem(phase, NUM_SLOTS)
+        @pl.when(near(step))
+        def _():
+            wait_offs(step)
+
+    def compute(phase):
+        slot = slot_of(phase)
         base = pair_base(phase)
         hidden = h_buf[piece_of(phase), pl.ds(pl.multiple_of(base * 4 * rows, half), half), :]
         offsets = []
@@ -242,24 +241,48 @@
         for l in range(2):
             acc[base + l, :, :] = sums[l]
 
-        @pl.when((phase < NUM_PIECES - NUM_SLOTS) | ((phase >= NUM_PIECES) & (phase < 2 * NUM_PIECES - NUM_SLOTS)))
+    def run_phase(phase, carry):
+        @pl.when(phase < NUM_PIECES - 2 * LEAD)
+        def _():
+            for copy in side_sends(phase + 2 * LEAD):
+                copy.start()
+
+        relay(phase + LEAD)
+        hop(phase + 1)
+        settle(phase)
+
+        @pl.when((phase < 7) | (phase == 13) | (phase == 14))
+        def _():
+            for copy in head_copies(phase):
+                copy.wait()
+
+        @pl.when(phase == 7)
+        def _():
+            for step in range(1, NUM_SHARDS):
+                @pl.when(jnp.logical_not(near(step)))
+                def _():
+                    wait_offs(step)
+
+        @pl.when(phase == num_phases - 1)
+        def _():
+            for step in range(1, NUM_SHARDS):
+                @pl.when(jnp.logical_not(near(step)))
+                def _():
+                    send_scores(step).start()
+
+        compute(phase)
+
+        @pl.when((phase == 0) | (phase == 7) | (phase == 8))
         def _():
             for copy in head_copies(phase + NUM_SLOTS):
                 copy.start(priority=1)
 
-        @pl.when(phase == NUM_PIECES)
-        def _():
-            for step in range(1, NUM_SHARDS):
-                @pl.when(near(step))
-                def _():
-                    send_scores(step).start()
-
         return carry
 
     lax.fori_loop(0, num_phases, run_phase, 0)
 
     for step in range(1, NUM_SHARDS):
-        @pl.when(jnp.logical_not(near(step)))
+        @pl.when(near(step))
         def _():
             send_scores(step).start()
     ret_in[me, :, :] = acc[z, :, :]

time: 64.6 us -> 65.7 us (1.017)
  Pallas kernels: 61.3 us -> 62.3 us
    pallas_call x1, Pallas kernels: 61.3 us -> 62.3 us  [local_step(): pl.pallas_call(functools.partial(kernel, shard_len, width, rows), out_sha...]
where the time goes in v3:
time: 65.7 us; the launch traced here: 65.4 us
  Pallas kernels  62.3 us (95%)
  local copies, waits for them, and re-layouts  2.46 us (4%)
    pallas_call x1, Pallas kernels, local_step(): pl.pallas_call(functools.partial(kernel, shard_len, width, rows), out_sha...  62.3 us
    unnamed x2, local copies, waits for them, and re-layouts  2.46 us

profile of v3, /device:TPU:0, one launch (start us, length us, event | category | flops | bytes accessed | tf_op | source)
XLA Modules:
  0.0 65.4 jit_solution(2654274997089324815)
XLA Ops:
  0.6 62.3 %shard_map.68 = (f32[32,32]{1,0:T(8,128)}, f32[1,32]{1,0:T(1,128)}) custom-call(s32[32]{0:T(128)} %tgt_hbm.1, s32[32,32]{1,0:T(8,128)} %ids_hbm.1, s32[32,32]{1,0:T(8,128)} %valid_hbm.1, bf16[32,4096]{1,0:T(8,128)(2,1)} %hidden_ref.1, bf16[8016,4096]{1,0:T(8,128)(2,1)} %head_ref.1), custom_call_target="tpu_custom_call" | custom-call | tf_op jit(solution)/shard_map/pallas_call | solution.py:357
  62.9 1.3 %copy.9 = f32[32,32]{1,0:T(8,128)} copy(f32[32,32]{1,0:T(8,128)} %get-tuple-element.8) | data formatting | bytes 8192
  64.3 1.1 %copy.10 = f32[32]{0:T(128)} copy(f32[32]{0:T(128)} %bitcast.1) | data formatting | bytes 256

commit v4 on v2

--- a/solution.py
+++ b/solution.py
@@ -16,13 +16,14 @@
 HEAD_BLOCK = 1008
 SLOT_CAP = 8
 LANES = 128
+FAR_FIRST = 1
 LEAD = 3
 
 
 def kernel(shard_len, width, rows,
            tgt_hbm, ids_hbm, valid_hbm, hidden_ref, head_ref,
-           p_hbm, lp_hbm,
-           tgt_ref, ids_ref, valid_ref, p_ref, lp_ref, small_sem,
+           p_ref, lp_ref,
+           tgt_ref, ids_ref, valid_ref, small_sem,
            head_buf, h_buf, square, turned, codes, offs_out, offs_in, acc, ret_in,
            head_sem, local_sem, recv_sem, own_sem, far_sem, relay_sem, hop_sem,
            offs_send, offs_recv, ret_send, ret_recv):
@@ -50,7 +51,7 @@
     blocks = [(start, min(HEAD_BLOCK, shard_len - start)) for start in range(0, shard_len, HEAD_BLOCK)]
 
     def piece_of(phase):
-        return lax.rem(phase + 2 * lax.div(phase, NUM_PIECES), NUM_PIECES)
+        return lax.rem(phase + (NUM_PIECES - NUM_SLOTS) * lax.div(phase, NUM_PIECES), NUM_PIECES)
 
     def head_copies(phase):
         cols = pl.ds(pl.multiple_of(piece_of(phase) * depth, depth), depth)
@@ -66,8 +67,6 @@
                     for k in range(NUM_PIECES)]
     small_copies = [pltpu.make_async_copy(src, dst, small_sem.at[i]) for i, (src, dst) in enumerate(
         ((ids_hbm, ids_ref), (valid_hbm, valid_ref), (tgt_hbm, tgt_ref)))]
-    out_copies = [pltpu.make_async_copy(src, dst, small_sem.at[3 + i]) for i, (src, dst) in enumerate(
-        ((p_ref, p_hbm), (lp_ref, lp_hbm)))]
     for copy in local_copies[:LEAD] + small_copies + local_copies[LEAD:]:
         copy.start()
     for phase in range(NUM_SLOTS):
@@ -187,6 +186,9 @@
         for copy in side_sends(LEAD + phase):
             copy.start()
     hop(0)
+    for i in range(FAR_FIRST):
+        for copy in far_sends(piece_of(NUM_PIECES + i)):
+            copy.start()
 
     def wait_offs(step):
         src = partner(step)
@@ -198,9 +200,9 @@
         wait_offs(step)
 
     def run_phase(phase, carry):
-        @pl.when(phase < NUM_PIECES)
-        def _():
-            for copy in far_sends(piece_of(phase + NUM_PIECES)):
+        @pl.when(phase < NUM_PIECES - FAR_FIRST)
+        def _():
+            for copy in far_sends(piece_of(phase + NUM_PIECES + FAR_FIRST)):
                 copy.start()
 
         relay(phase + LEAD)
@@ -309,14 +311,10 @@
     top = jnp.max(logits, axis=1, keepdims=True)
     log_norm = top + jnp.log(jnp.sum(jnp.exp(logits - top), axis=1, keepdims=True))
     p_ref[...] = jnp.where(is_valid, jnp.exp(logits - log_norm), 0.0)
-    out_copies[0].start()
     col_pos = lax.broadcasted_iota(jnp.int32, (rows, 32), 1)
     chosen = jnp.sum(jnp.where(col_pos == target, logits, 0.0), axis=1, keepdims=True)
     turned[0:rows, :] = jnp.broadcast_to(chosen - log_norm, (rows, LANES))
     lp_ref[...] = jnp.transpose(turned[...])[0:1, 0:rows]
-    out_copies[1].start()
-    for copy in out_copies:
-        copy.wait()
 
 
 def solution(mesh):
@@ -333,16 +331,14 @@
         tile = (SLOT_CAP, LANES)
         p, lp = pl.pallas_call(
             functools.partial(kernel, shard_len, width, rows),
-            out_shape=(jax.ShapeDtypeStruct((rows, 32), jnp.float32), jax.ShapeDtypeStruct((1, rows), jnp.float32)),
+            out_shape=(pltpu.VMEM((rows, 32), jnp.float32), pltpu.VMEM((1, rows), jnp.float32)),
             in_specs=[pl.BlockSpec(memory_space=pl.ANY)] * 5,
-            out_specs=(pl.BlockSpec(memory_space=pl.ANY),) * 2,
+            out_specs=(pl.BlockSpec(memory_space=pltpu.VMEM),) * 2,
             scratch_shapes=[
                 pltpu.SMEM((rows,), jnp.int32),
                 pltpu.VMEM((rows, 32), jnp.int32),
                 pltpu.VMEM((rows, 32), jnp.int32),
-                pltpu.VMEM((rows, 32), jnp.float32),
-                pltpu.VMEM((1, rows), jnp.float32),
-                dma((5,)),
+                dma((3,)),
                 pltpu.VMEM((NUM_SLOTS, shard_len, depth), jnp.bfloat16),
                 pltpu.VMEM((NUM_PIECES, NUM_SHARDS * rows, depth), jnp.bfloat16),
                 pltpu.VMEM((LANES, LANES), jnp.int32),
@@ -356,7 +352,7 @@
                 dma((3, NUM_PIECES)), dma((2, NUM_PIECES)), dma((2, 2, 2 * NUM_PIECES)), dma((2, 2 * NUM_PIECES)),
                 dma((NUM_SHARDS,)), dma((NUM_SHARDS,)), dma((NUM_SHARDS,)), dma((NUM_SHARDS,)),
             ],
-            compiler_params=pltpu.CompilerParams(collective_id=0, has_side_effects=True, vmem_limit_bytes=67043328),
+            compiler_params=pltpu.CompilerParams(collective_id=0, has_side_effects=True, vmem_limit_bytes=62 * 2**20),
         )(target_pos, allowed_ids, valid_mask, hidden, head_rows)
         return p, lp.reshape(rows)
 

time: 64.6 us -> 62.6 us (0.969)
  local copies, waits for them, and re-layouts: 2.46 us -> 1.12 us
    unnamed x2, local copies, waits for them, and re-layouts: 2.46 us -> 1.12 us
where the time goes in v4:
time: 62.6 us; the launch traced here: 62.4 us
  Pallas kernels  60.7 us (97%)
  local copies, waits for them, and re-layouts  1.12 us (2%)
  between operations  0.64 us (1%)
    pallas_call x1, Pallas kernels, local_step(): pl.pallas_call(functools.partial(kernel, shard_len, width, rows), out_sha...  60.7 us

profile of v4, /device:TPU:0, one launch (start us, length us, event | category | flops | bytes accessed | tf_op | source)
XLA Modules:
  0.0 62.4 jit_solution(3884023039237483027)
XLA Ops:
  0.6 60.7 %shard_map.68 = (f32[32,32]{1,0:T(8,128)S(1)}, f32[1,32]{1,0:T(1,128)S(1)}) custom-call(s32[32]{0:T(128)} %tgt_hbm.1, s32[32,32]{1,0:T(8,128)} %ids_hbm.1, s32[32,32]{1,0:T(8,128)} %valid_hbm.1, bf16[32,4096]{1,0:T(8,128)(2,1)} %hidden_ref.1, bf16[8016,4096]{1,0:T(8,128)(2,1)} %head_ref.1), custom_call_target="tpu_custom_call" | custom-call | tf_op jit(solution)/shard_map/pallas_call | solution.py:332
  61.3 0.6 copy.9
  61.9 0.5 copy.10

commit v5 on v4

--- a/solution.py
+++ b/solution.py
@@ -14,6 +14,7 @@
 NUM_PIECES = 8
 NUM_SLOTS = 6
 HEAD_BLOCK = 1008
+HEAD_LOAD = 2016
 SLOT_CAP = 8
 LANES = 128
 FAR_FIRST = 1
@@ -49,6 +50,7 @@
         pl.semaphore_signal(barrier, inc=1, device_id=device(partner(step)), device_id_type=MESH)
 
     blocks = [(start, min(HEAD_BLOCK, shard_len - start)) for start in range(0, shard_len, HEAD_BLOCK)]
+    loads = [(start, min(HEAD_LOAD, shard_len - start)) for start in range(0, shard_len, HEAD_LOAD)]
 
     def piece_of(phase):
         return lax.rem(phase + (NUM_PIECES - NUM_SLOTS) * lax.div(phase, NUM_PIECES), NUM_PIECES)
@@ -58,7 +60,7 @@
         slot = lax.rem(phase, NUM_SLOTS)
         return [pltpu.make_async_copy(head_ref.at[pl.ds(start, size), cols],
                                       head_buf.at[slot, pl.ds(start, size), :], head_sem.at[slot, i])
-                for i, (start, size) in enumerate(blocks)]
+                for i, (start, size) in enumerate(loads)]
 
     def block_of(shard, piece):
         return h_buf.at[piece, pl.ds(pl.multiple_of(shard * rows, rows), rows), :]
@@ -183,6 +185,7 @@
         line_send(k).start()
     for phase in range(LEAD):
         relay(phase)
+    for phase in range(LEAD):
         for copy in side_sends(LEAD + phase):
             copy.start()
     hop(0)

time: 62.6 us -> 62.5 us (level)
  no operation moved by 1% of the time
where the time goes in v5:
time: 62.5 us; the launch traced here: 62.3 us
  Pallas kernels  60.6 us (97%)
  local copies, waits for them, and re-layouts  1.12 us (2%)
  between operations  0.64 us (1%)
    pallas_call x1, Pallas kernels, local_step(): pl.pallas_call(functools.partial(kernel, shard_len, width, rows), out_sha...  60.6 us

profile of v5, /device:TPU:0, one launch (start us, length us, event | category | flops | bytes accessed | tf_op | source)
XLA Modules:
  0.0 62.3 jit_solution(4243240109574386243)
XLA Ops:
  0.6 60.6 %shard_map.68 = (f32[32,32]{1,0:T(8,128)S(1)}, f32[1,32]{1,0:T(1,128)S(1)}) custom-call(s32[32]{0:T(128)} %tgt_hbm.1, s32[32,32]{1,0:T(8,128)} %ids_hbm.1, s32[32,32]{1,0:T(8,128)} %valid_hbm.1, bf16[32,4096]{1,0:T(8,128)(2,1)} %hidden_ref.1, bf16[8016,4096]{1,0:T(8,128)(2,1)} %head_ref.1), custom_call_target="tpu_custom_call" | custom-call | tf_op jit(solution)/shard_map/pallas_call | solution.py:335
  61.2 0.6 copy.9
  61.8 0.5 copy.10
